TPU v7x, 128 devices: a whole 4x4x4 slice. The times are simulated.
128 devices in a mesh: row: 8 (over x, core), col: 16 (over y, z).
Axes of the slice: x: 4, y: 4, z: 4, core: 2. Of those that a mesh axis runs over, the one named last changes fastest.
Arguments:
- tiles: bfloat16 [8, 16, 128, 128, 128], P('row', 'col')
- tile_row: int32 [8, 16, 128], P('row', 'col'), may hold values from 0 to 15, as said below
- tile_col: int32 [8, 16, 128], P('row', 'col'), may hold values from 0 to 15
- tile_count: int32 [8, 16], P('row', 'col'), may hold values from 1 to 128, as said below
- sinogram: float32 [8, 2048, 128], P('row', 'col')
Outputs:
- volume: float32 [16, 2048, 128], P('col', 'row')
- residual: float32 [8, 2048, 128], P('row', 'col')
Inputs may be any that keep to these rules, and one draw needn't show every extreme that they name: Within one block the pairs (tile_row, tile_col) of all 128 slots are distinct. Slots 0 to tile_count - 1 of a block are live, the rest are ignored; some block has all 128 slots live in every draw.
All inputs are finite; a program needn't handle non-finite values.
Results may differ from a plain program's by a relative error of at most 0.015.
Values may be sent and summed in bfloat16 or wider, within the bound.
A program may use at most 64 MiB of HBM per device.

v0:
```python
import functools

import jax
import jax.numpy as jnp
from jax import lax
from jax.sharding import Mesh
from jax.sharding import PartitionSpec as P

RT = 16
VT = 16
ITERS = 4
ROW = ("row_0", "row_1")
COL = ("col_0", "col_1")
ROW_COL = ("row_0", "row_1", "col_0", "col_1")


def sent_to_all(shard, axis):
    copies = jnp.broadcast_to(shard, (lax.axis_size(axis), *shard.shape))
    return lax.all_to_all(copies, axis, split_axis=0, concat_axis=0, tiled=True)


def joined_along(parts, dim):
    dims = list(parts.shape[1:])
    dims[dim] *= parts.shape[0]
    return jnp.moveaxis(parts, 0, dim).reshape(dims)


def collect(shard, axis, dim):
    parts = sent_to_all(shard, axis)
    return joined_along(parts, dim)


def in_blocks(shard, dim, peers):
    before, after = (shard.shape[:dim], shard.shape[dim + 1 :])
    return jnp.moveaxis(shard.reshape(*before, peers, -1, *after), dim, 0)


def sum_at_owner(shard, axis, dim):
    parts = in_blocks(shard, dim, lax.axis_size(axis))
    arrived = lax.all_to_all(parts, axis, split_axis=0, concat_axis=0, tiled=True)
    return arrived.sum(axis=0)


def by_axis(shard, axes):
    return functools.reduce(lax.psum, axes, shard)


def frame_squares(values):
    return jnp.sum(values * values, axis=(0, 1))


def forward_local(blocks, rows_index, cols_index, count, voxel_block):
    tile = blocks.shape[1]
    frames = voxel_block.shape[1]
    voxel_tiles = voxel_block.reshape(voxel_block.shape[0] // tile, tile, frames)
    picked = jnp.take(voxel_tiles, cols_index, axis=0)
    products = jnp.einsum("tij,tjk->tik", blocks, picked, preferred_element_type=jnp.float32)
    live = jnp.arange(blocks.shape[0], dtype=jnp.int32) < count
    select = (
        (rows_index[None, :] == jnp.arange(RT, dtype=jnp.int32)[:, None]) & live[None, :]
    ).astype(jnp.float32)
    summed = jnp.einsum("ut,tik->uik", select, products, precision=lax.Precision.HIGHEST)
    return summed.reshape(RT * tile, frames)


def backward_local(blocks, rows_index, cols_index, count, ray_block):
    tile = blocks.shape[1]
    frames = ray_block.shape[1]
    ray_tiles = ray_block.reshape(ray_block.shape[0] // tile, tile, frames)
    picked = jnp.take(ray_tiles, rows_index, axis=0)
    products = jnp.einsum("tji,tjk->tik", blocks, picked, preferred_element_type=jnp.float32)
    live = jnp.arange(blocks.shape[0], dtype=jnp.int32) < count
    select = (
        (cols_index[None, :] == jnp.arange(VT, dtype=jnp.int32)[:, None]) & live[None, :]
    ).astype(jnp.float32)
    summed = jnp.einsum("ut,tik->uik", select, products, precision=lax.Precision.HIGHEST)
    return summed.reshape(VT * tile, frames)


def local(tiles, tile_row, tile_col, tile_count, sinogram):
    blocks = tiles[0, 0]
    rows_index = tile_row[0, 0]
    cols_index = tile_col[0, 0]
    count = tile_count[0, 0]
    tile = blocks.shape[1]
    frames = sinogram.shape[2]
    voxel_piece = VT * tile // lax.axis_size(ROW)

    def ray_block_of(state):
        return collect(state.astype(jnp.bfloat16), COL, 1)[0]

    def voxel_total(term):
        return sum_at_owner(term, ROW, 1)

    residual = sinogram
    volume = jnp.zeros((1, voxel_piece, frames), jnp.float32)

    def backward(state):
        return voxel_total(
            backward_local(blocks, rows_index, cols_index, count, ray_block_of(state))[None]
        )

    search = backward(residual)
    gamma = by_axis(frame_squares(search), ROW_COL)
    direction = search
    for step in range(ITERS):
        image = sum_at_owner(
            forward_local(
                blocks,
                rows_index,
                cols_index,
                count,
                collect(direction.astype(jnp.bfloat16), ROW, 1)[0],
            )[None],
            COL,
            1,
        )
        alpha = gamma / by_axis(frame_squares(image), ROW_COL)
        volume = volume + alpha * direction
        residual = residual - alpha * image
        if step + 1 < ITERS:
            search = backward(residual)
            fresh = by_axis(frame_squares(search), ROW_COL)
            direction = search + fresh / gamma * direction
            gamma = fresh
    return (volume, residual)


def solution(mesh):
    finer = Mesh(mesh.devices.reshape(4, 2, 4, 4), ("row_0", "row_1", "col_0", "col_1"))
    placed = (
        P(ROW, COL, None, None, None),
        P(ROW, COL, None),
        P(ROW, COL, None),
        P(ROW, COL),
        P(ROW, COL, None),
    )
    return jax.shard_map(
        local,
        mesh=finer,
        in_specs=placed,
        out_specs=(P(COL, ROW, None), P(ROW, COL, None)),
        check_vma=False,
    )
```

profile of v0, /device:TPU:1, one launch (start us, length us, event | category | flops | bytes accessed | tf_op | source)
XLA Modules:
  0.0 684.5 jit_solution(11799658485803393305)
XLA Ops:
  2.4 8.6 %all-to-all-start = ((bf16[16,1,128,128]{3,2,1,0:T(8,128)(2,1)}), bf16[16,1,128,128]{3,2,1,0:T(8,128)(2,1)S(1)}, u32[]{:S(2)}, u32[]{:S(2)}) async-start(bf16[16,1,128,128]{3,2,1,0:T(8,128)(2,1)} %broadcast_in_dim.25), calls=%async_computation | async-start | bytes 1048576 | tf_op jit(solution)/shard_map/all_to_all | solution.py:19
  13.0 8.4 %all-to-all-done = bf16[16,1,128,128]{3,2,1,0:T(8,128)(2,1)S(1)} async-done(((bf16[16,1,128,128]{3,2,1,0:T(8,128)(2,1)}), bf16[16,1,128,128]{3,2,1,0:T(8,128)(2,1)S(1)}, u32[]{:S(2)}, u32[]{:S(2)}) %all-to-all-start) | async-done | bytes 524320 | tf_op jit(solution)/shard_map/all_to_all | solution.py:19
  24.4 8.4 %fusion.32 = f32[128,128,128]{1,2,0:T(8,128)} fusion(bf16[1,1,128,128,128]{4,3,2,1,0:T(8,128)(2,1)} %param.7, bf16[128,128,128]{2,1,0:T(8,128)(2,1)} %gather_fusion, pred[128]{0:T(512)(128)(4,1)S(1)} %compare_and_fusion.1), kind=kOutput, calls=%fused_computation.40 | convolution fusion | flops 538968064 | bytes 16777344 | tf_op jit(solution)/shard_map/tji,tjk->tik/dot_general | solution.py:71
  32.8 9.3 %copy.60 = f32[128,128,128]{2,0,1:T(8,128)} copy(f32[128,128,128]{1,2,0:T(8,128)} %fusion.32) | data formatting | bytes 16777216 | tf_op jit(solution)/shard_map/tji,tjk->tik/dot_general | solution.py:71
  47.5 21.1 %all_to_all.80 = f32[8,1,256,128]{3,2,1,0:T(8,128)S(1)} all-to-all(f32[8,1,256,128]{3,2,1,0:T(8,128)S(1)} %bitcast.176), channel_id=1, replica_groups=mesh['row_0'=4,'row_1'=2,'col_0'=4,'col_1'=4] {'row_0','row_1'}, dimensions={0} | all-to-all | bytes 2097152 | tf_op jit(solution)/shard_map/all_to_all | solution.py:40
  74.1 9.4 %all-to-all-done.2 = bf16[8,1,256,128]{3,2,1,0:T(8,128)(2,1)S(1)} async-done(((bf16[8,1,256,128]{3,2,1,0:T(8,128)(2,1)}), bf16[8,1,256,128]{3,2,1,0:T(8,128)(2,1)S(1)}, u32[]{:S(2)}, u32[]{:S(2)}) %all-to-all-start.2) | async-done | bytes 524320 | tf_op jit(solution)/shard_map/all_to_all | solution.py:19
  86.5 9.9 %fusion.37 = f32[128,128,128]{1,2,0:T(8,128)} fusion(bf16[1,1,128,128,128]{4,3,2,1,0:T(8,128)(2,1)} %param.7, bf16[128,128,128]{2,1,0:T(8,128)(2,1)} %gather_fusion.1, pred[128]{0:T(512)(128)(4,1)S(1)} %compare_and_fusion), kind=kOutput, calls=%fused_computation.41 | convolution fusion | flops 538968064 | bytes 16777344 | tf_op jit(solution)/shard_map/tij,tjk->tik/dot_general | solution.py:57
  96.4 9.3 %copy.64 = f32[128,128,128]{2,0,1:T(8,128)} copy(f32[128,128,128]{1,2,0:T(8,128)} %fusion.37) | data formatting | bytes 16777216 | tf_op jit(solution)/shard_map/tij,tjk->tik/dot_general | solution.py:57
  111.2 18.7 %all_to_all.81 = f32[16,1,128,128]{3,2,1,0:T(8,128)S(1)} all-to-all(f32[16,1,128,128]{3,2,1,0:T(8,128)S(1)} %copy.65), channel_id=1, replica_groups=mesh['row_0'=4,'row_1'=2,'col_0'=4,'col_1'=4] {'col_0','col_1'}, dimensions={0} | all-to-all | bytes 2097152 | tf_op jit(solution)/shard_map/all_to_all | solution.py:40
  130.0 6.9 %all-reduce.2 = (f32[128]{0:T(128)S(1)}, f32[128]{0:T(128)S(1)}) all-reduce(f32[128]{0:T(128)S(1)} %get-tuple-element.15, f32[128]{0:T(128)S(1)} %multiply_reduce_fusion.7), channel_id=1, replica_groups=mesh['row_0'=4,'row_1'=2,'col_0'=4,'col_1'=4] {'row_0'}, use_global_device_ids=true, to_apply=%region_2.4 | all-reduce | flops 256 | bytes 2048 | tf_op jit(solution)/shard_map/psum | solution.py:45
  143.4 6.8 all-reduce.1
  156.6 11.9 %all_to_all.82 = bf16[16,1,128,128]{3,2,1,0:T(8,128)(2,1)S(1)} all-to-all(bf16[16,1,128,128]{3,2,1,0:T(8,128)(2,1)S(1)} %broadcast_in_dim.27), channel_id=1, replica_groups=mesh['row_0'=4,'row_1'=2,'col_0'=4,'col_1'=4] {'col_0','col_1'}, dimensions={0} | all-to-all | bytes 1048576 | tf_op jit(solution)/shard_map/all_to_all | solution.py:19
  171.5 8.4 %fusion.42 = f32[128,128,128]{1,2,0:T(8,128)} fusion(bf16[1,1,128,128,128]{4,3,2,1,0:T(8,128)(2,1)} %param.7, bf16[128,128,128]{2,1,0:T(8,128)(2,1)} %gather_fusion.2, pred[128]{0:T(512)(128)(4,1)S(1)} %compare_and_fusion.1), kind=kOutput, calls=%fused_computation.42 | convolution fusion | flops 538968064 | bytes 16777344 | tf_op jit(solution)/shard_map/tji,tjk->tik/dot_general | solution.py:71
  179.9 9.3 %copy.67 = f32[128,128,128]{2,0,1:T(8,128)} copy(f32[128,128,128]{1,2,0:T(8,128)} %fusion.42) | data formatting | bytes 16777216 | tf_op jit(solution)/shard_map/tji,tjk->tik/dot_general | solution.py:71
  194.7 23.1 %all_to_all.83 = f32[8,1,256,128]{3,2,1,0:T(8,128)S(1)} all-to-all(f32[8,1,256,128]{3,2,1,0:T(8,128)S(1)} %bitcast.177), channel_id=1, replica_groups=mesh['row_0'=4,'row_1'=2,'col_0'=4,'col_1'=4] {'row_0','row_1'}, dimensions={0} | all-to-all | bytes 2097152 | tf_op jit(solution)/shard_map/all_to_all | solution.py:40
  217.9 6.9 %psum.232 = f32[128]{0:T(128)S(1)} all-reduce(f32[128]{0:T(128)S(1)} %multiply_reduce_fusion.2), channel_id=1, replica_groups=mesh['row_0'=4,'row_1'=2,'col_0'=4,'col_1'=4] {'row_0'}, use_global_device_ids=true, to_apply=%region_14.16 | all-reduce | flops 128 | bytes 1024 | tf_op jit(solution)/shard_map/psum | solution.py:45
  229.9 6.8 psum.234
  243.1 16.1 %all_to_all.84 = bf16[8,1,256,128]{3,2,1,0:T(8,128)(2,1)S(1)} all-to-all(bf16[8,1,256,128]{3,2,1,0:T(8,128)(2,1)S(1)} %broadcast_in_dim.28), channel_id=1, replica_groups=mesh['row_0'=4,'row_1'=2,'col_0'=4,'col_1'=4] {'row_0','row_1'}, dimensions={0} | all-to-all | bytes 1048576 | tf_op jit(solution)/shard_map/all_to_all | solution.py:19
  262.3 9.9 %fusion.47 = f32[128,128,128]{1,2,0:T(8,128)} fusion(bf16[1,1,128,128,128]{4,3,2,1,0:T(8,128)(2,1)} %param.7, bf16[128,128,128]{2,1,0:T(8,128)(2,1)} %gather_fusion.3, pred[128]{0:T(512)(128)(4,1)S(1)} %compare_and_fusion), kind=kOutput, calls=%fused_computation.43 | convolution fusion | flops 538968064 | bytes 16777344 | tf_op jit(solution)/shard_map/tij,tjk->tik/dot_general | solution.py:57
  272.2 9.3 %copy.71 = f32[128,128,128]{2,0,1:T(8,128)} copy(f32[128,128,128]{1,2,0:T(8,128)} %fusion.47) | data formatting | bytes 16777216 | tf_op jit(solution)/shard_map/tij,tjk->tik/dot_general | solution.py:57
  287.0 18.2 %all_to_all.85 = f32[16,1,128,128]{3,2,1,0:T(8,128)S(1)} all-to-all(f32[16,1,128,128]{3,2,1,0:T(8,128)S(1)} %copy.72), channel_id=1, replica_groups=mesh['row_0'=4,'row_1'=2,'col_0'=4,'col_1'=4] {'col_0','col_1'}, dimensions={0} | all-to-all | bytes 2097152 | tf_op jit(solution)/shard_map/all_to_all | solution.py:40
  305.2 6.9 %psum.236 = f32[128]{0:T(128)S(1)} all-reduce(f32[128]{0:T(128)S(1)} %multiply_reduce_fusion.6), channel_id=1, replica_groups=mesh['row_0'=4,'row_1'=2,'col_0'=4,'col_1'=4] {'row_0'}, use_global_device_ids=true, to_apply=%region_20.22 | all-reduce | flops 128 | bytes 1024 | tf_op jit(solution)/shard_map/psum | solution.py:45
  318.8 6.8 psum.238
  325.5 6.7 psum.239
  332.4 11.7 %all_to_all.86 = bf16[16,1,128,128]{3,2,1,0:T(8,128)(2,1)S(1)} all-to-all(bf16[16,1,128,128]{3,2,1,0:T(8,128)(2,1)S(1)} %broadcast_in_dim.29), channel_id=1, replica_groups=mesh['row_0'=4,'row_1'=2,'col_0'=4,'col_1'=4] {'col_0','col_1'}, dimensions={0} | all-to-all | bytes 1048576 | tf_op jit(solution)/shard_map/all_to_all | solution.py:19
  347.2 8.4 %fusion.52 = f32[128,128,128]{1,2,0:T(8,128)} fusion(bf16[1,1,128,128,128]{4,3,2,1,0:T(8,128)(2,1)} %param.7, bf16[128,128,128]{2,1,0:T(8,128)(2,1)} %gather_fusion.4, pred[128]{0:T(512)(128)(4,1)S(1)} %compare_and_fusion.1), kind=kOutput, calls=%fused_computation.44 | convolution fusion | flops 538968064 | bytes 16777344 | tf_op jit(solution)/shard_map/tji,tjk->tik/dot_general | solution.py:71
  355.5 9.3 %copy.74 = f32[128,128,128]{2,0,1:T(8,128)} copy(f32[128,128,128]{1,2,0:T(8,128)} %fusion.52) | data formatting | bytes 16777216 | tf_op jit(solution)/shard_map/tji,tjk->tik/dot_general | solution.py:71
  370.3 23.1 %all_to_all.87 = f32[8,1,256,128]{3,2,1,0:T(8,128)S(1)} all-to-all(f32[8,1,256,128]{3,2,1,0:T(8,128)S(1)} %bitcast.178), channel_id=1, replica_groups=mesh['row_0'=4,'row_1'=2,'col_0'=4,'col_1'=4] {'row_0','row_1'}, dimensions={0} | all-to-all | bytes 2097152 | tf_op jit(solution)/shard_map/all_to_all | solution.py:40
  393.5 6.9 %psum.240 = f32[128]{0:T(128)S(1)} all-reduce(f32[128]{0:T(128)S(1)} %multiply_reduce_fusion.1), channel_id=1, replica_groups=mesh['row_0'=4,'row_1'=2,'col_0'=4,'col_1'=4] {'row_0'}, use_global_device_ids=true, to_apply=%region_26.28 | all-reduce | flops 128 | bytes 1024 | tf_op jit(solution)/shard_map/psum | solution.py:45
  405.5 6.8 psum.242
  418.8 16.1 %all_to_all.88 = bf16[8,1,256,128]{3,2,1,0:T(8,128)(2,1)S(1)} all-to-all(bf16[8,1,256,128]{3,2,1,0:T(8,128)(2,1)S(1)} %broadcast_in_dim.30), channel_id=1, replica_groups=mesh['row_0'=4,'row_1'=2,'col_0'=4,'col_1'=4] {'row_0','row_1'}, dimensions={0} | all-to-all | bytes 1048576 | tf_op jit(solution)/shard_map/all_to_all | solution.py:19
  437.9 9.9 %fusion.57 = f32[128,128,128]{1,2,0:T(8,128)} fusion(bf16[1,1,128,128,128]{4,3,2,1,0:T(8,128)(2,1)} %param.7, bf16[128,128,128]{2,1,0:T(8,128)(2,1)} %gather_fusion.5, pred[128]{0:T(512)(128)(4,1)S(1)} %compare_and_fusion), kind=kOutput, calls=%fused_computation.45 | convolution fusion | flops 538968064 | bytes 16777344 | tf_op jit(solution)/shard_map/tij,tjk->tik/dot_general | solution.py:57
  447.8 9.3 %copy.78 = f32[128,128,128]{2,0,1:T(8,128)} copy(f32[128,128,128]{1,2,0:T(8,128)} %fusion.57) | data formatting | bytes 16777216 | tf_op jit(solution)/shard_map/tij,tjk->tik/dot_general | solution.py:57
  462.6 18.2 %all_to_all.89 = f32[16,1,128,128]{3,2,1,0:T(8,128)S(1)} all-to-all(f32[16,1,128,128]{3,2,1,0:T(8,128)S(1)} %copy.79), channel_id=1, replica_groups=mesh['row_0'=4,'row_1'=2,'col_0'=4,'col_1'=4] {'col_0','col_1'}, dimensions={0} | all-to-all | bytes 2097152 | tf_op jit(solution)/shard_map/all_to_all | solution.py:40
  480.9 6.9 %psum.244 = f32[128]{0:T(128)S(1)} all-reduce(f32[128]{0:T(128)S(1)} %multiply_reduce_fusion.5), channel_id=1, replica_groups=mesh['row_0'=4,'row_1'=2,'col_0'=4,'col_1'=4] {'row_0'}, use_global_device_ids=true, to_apply=%region_32.34 | all-reduce | flops 128 | bytes 1024 | tf_op jit(solution)/shard_map/psum | solution.py:45
  494.4 6.8 psum.246
  507.8 11.7 %all_to_all.90 = bf16[16,1,128,128]{3,2,1,0:T(8,128)(2,1)S(1)} all-to-all(bf16[16,1,128,128]{3,2,1,0:T(8,128)(2,1)S(1)} %broadcast_in_dim.31), channel_id=1, replica_groups=mesh['row_0'=4,'row_1'=2,'col_0'=4,'col_1'=4] {'col_0','col_1'}, dimensions={0} | all-to-all | bytes 1048576 | tf_op jit(solution)/shard_map/all_to_all | solution.py:19
  522.6 8.4 %fusion.62 = f32[128,128,128]{1,2,0:T(8,128)} fusion(bf16[1,1,128,128,128]{4,3,2,1,0:T(8,128)(2,1)} %param.7, bf16[128,128,128]{2,1,0:T(8,128)(2,1)} %gather_fusion.6, pred[128]{0:T(512)(128)(4,1)S(1)} %compare_and_fusion.1), kind=kOutput, calls=%fused_computation.46 | convolution fusion | flops 538968064 | bytes 16777344 | tf_op jit(solution)/shard_map/tji,tjk->tik/dot_general | solution.py:71
  530.9 9.3 %copy.81 = f32[128,128,128]{2,0,1:T(8,128)} copy(f32[128,128,128]{1,2,0:T(8,128)} %fusion.62) | data formatting | bytes 16777216 | tf_op jit(solution)/shard_map/tji,tjk->tik/dot_general | solution.py:71
  545.7 23.1 %all_to_all.91 = f32[8,1,256,128]{3,2,1,0:T(8,128)S(1)} all-to-all(f32[8,1,256,128]{3,2,1,0:T(8,128)S(1)} %bitcast.179), channel_id=1, replica_groups=mesh['row_0'=4,'row_1'=2,'col_0'=4,'col_1'=4] {'row_0','row_1'}, dimensions={0} | all-to-all | bytes 2097152 | tf_op jit(solution)/shard_map/all_to_all | solution.py:40
  568.9 6.9 %psum.248 = f32[128]{0:T(128)S(1)} all-reduce(f32[128]{0:T(128)S(1)} %multiply_reduce_fusion), channel_id=1, replica_groups=mesh['row_0'=4,'row_1'=2,'col_0'=4,'col_1'=4] {'row_0'}, use_global_device_ids=true, to_apply=%region_38.40 | all-reduce | flops 128 | bytes 1024 | tf_op jit(solution)/shard_map/psum | solution.py:45
  580.9 6.8 psum.250
  594.1 16.1 %all_to_all.92 = bf16[8,1,256,128]{3,2,1,0:T(8,128)(2,1)S(1)} all-to-all(bf16[8,1,256,128]{3,2,1,0:T(8,128)(2,1)S(1)} %broadcast_in_dim.32), channel_id=1, replica_groups=mesh['row_0'=4,'row_1'=2,'col_0'=4,'col_1'=4] {'row_0','row_1'}, dimensions={0} | all-to-all | bytes 1048576 | tf_op jit(solution)/shard_map/all_to_all | solution.py:19
  613.3 9.9 %fusion.67 = f32[128,128,128]{1,2,0:T(8,128)} fusion(bf16[1,1,128,128,128]{4,3,2,1,0:T(8,128)(2,1)} %param.7, bf16[128,128,128]{2,1,0:T(8,128)(2,1)} %gather_fusion.7, pred[128]{0:T(512)(128)(4,1)S(1)} %compare_and_fusion), kind=kOutput, calls=%fused_computation.47 | convolution fusion | flops 538968064 | bytes 16777344 | tf_op jit(solution)/shard_map/tij,tjk->tik/dot_general | solution.py:57
  623.2 9.3 %copy.85 = f32[128,128,128]{2,0,1:T(8,128)} copy(f32[128,128,128]{1,2,0:T(8,128)} %fusion.67) | data formatting | bytes 16777216 | tf_op jit(solution)/shard_map/tij,tjk->tik/dot_general | solution.py:57
  638.0 18.2 %all_to_all.93 = f32[16,1,128,128]{3,2,1,0:T(8,128)S(1)} all-to-all(f32[16,1,128,128]{3,2,1,0:T(8,128)S(1)} %copy.86), channel_id=1, replica_groups=mesh['row_0'=4,'row_1'=2,'col_0'=4,'col_1'=4] {'col_0','col_1'}, dimensions={0} | all-to-all | bytes 2097152 | tf_op jit(solution)/shard_map/all_to_all | solution.py:40
  656.3 6.9 %psum.252 = f32[128]{0:T(128)S(1)} all-reduce(f32[128]{0:T(128)S(1)} %multiply_reduce_fusion.4), channel_id=1, replica_groups=mesh['row_0'=4,'row_1'=2,'col_0'=4,'col_1'=4] {'row_0'}, use_global_device_ids=true, to_apply=%region_44.46 | all-reduce | flops 128 | bytes 1024 | tf_op jit(solution)/shard_map/psum | solution.py:45
  669.8 6.8 psum.254
  (91 shorter events, 159.8 us)
Async XLA Ops:
  2.4 19.0 %all-to-all-start = ((bf16[16,1,128,128]{3,2,1,0:T(8,128)(2,1)}), bf16[16,1,128,128]{3,2,1,0:T(8,128)(2,1)S(1)}, u32[]{:S(2)}, u32[]{:S(2)}) async-start(bf16[16,1,128,128]{3,2,1,0:T(8,128)(2,1)} %broadcast_in_dim.25), calls=%async_computation | async-start | bytes 1048576 | tf_op jit(solution)/shard_map/all_to_all | solution.py:19
  32.8 9.3 %copy-start.1 = (s32[1,1,128]{2,1,0:T(1,128)S(1)}, s32[1,1,128]{2,1,0:T(1,128)}, u32[]{:S(2)}) copy-start(s32[1,1,128]{2,1,0:T(1,128)} %param.9) | copy-start | bytes 1540
  69.6 13.8 %all-to-all-start.2 = ((bf16[8,1,256,128]{3,2,1,0:T(8,128)(2,1)}), bf16[8,1,256,128]{3,2,1,0:T(8,128)(2,1)S(1)}, u32[]{:S(2)}, u32[]{:S(2)}) async-start(bf16[8,1,256,128]{3,2,1,0:T(8,128)(2,1)} %broadcast_in_dim.26), calls=%async_computation.2 | async-start | bytes 1048576 | tf_op jit(solution)/shard_map/all_to_all | solution.py:19
  96.4 9.3 %copy-start.2 = (s32[1,1,128]{2,1,0:T(1,128)S(1)}, s32[1,1,128]{2,1,0:T(1,128)}, u32[]{:S(2)}) copy-start(s32[1,1,128]{2,1,0:T(1,128)} %param.8) | copy-start | bytes 1540
  110.8 45.6 %copy-start = (f32[1,128,128]{2,1,0:T(8,128)S(1)}, f32[1,128,128]{2,1,0:T(8,128)}, u32[]{:S(2)}) copy-start(f32[1,128,128]{2,1,0:T(8,128)} %param.11) | copy-start | bytes 196612
where the time goes:
time: 698 us; the launch traced here: 684 us
  blocking collectives  430 us (62%)
  matrix products  114 us (16%)
  local copies, waits for them, and re-layouts  104 us (15%)
  waiting for transfers between devices  17.7 us (3%)
  starting transfers between devices  13 us (2%)
    psum x28, blocking collectives, by_axis(): return functools.reduce(lax.psum, axes, shard)  182 us
    all_to_all x8, blocking collectives, sum_at_owner(): lax.all_to_all(parts, axis, split_axis=0, concat_axis=0, tiled=True)  164 us
    all_to_all x6, blocking collectives, sent_to_all(): return lax.all_to_all(copies, axis, split_axis=0, concat_axis=0, tiled=True)  83.6 us
    dot_general x4, matrix products, forward_local(): jnp.einsum('tij,tjk->tik', blocks, picked, preferred_element_type=jnp.flo...  39.6 us
    dot_general x4, local copies, waits for them, and re-layouts, backward_local(): jnp.einsum('tji,tjk->tik', blocks, picked, preferred_element_type=jnp.flo...  37.1 us
    dot_general x4, local copies, waits for them, and re-layouts, forward_local(): jnp.einsum('tij,tjk->tik', blocks, picked, preferred_element_type=jnp.flo...  37.1 us
    dot_general x4, matrix products, backward_local(): jnp.einsum('tji,tjk->tik', blocks, picked, preferred_element_type=jnp.flo...  33.5 us
    dot_general x4, matrix products, backward_local(): jnp.einsum('ut,tik->uik', select, products, precision=lax.Precision.HIGHEST)  20.6 us
  transfers between devices with their start and end apart: 2, of which 2 were waited for; matrix products, arithmetic and copies ran while one was open for 0% of the time, Pallas kernels for 0%

commit v1 on v0

v1 whole, which is shorter than its diff:
```python
import functools

import jax
import jax.numpy as jnp
from jax import lax
from jax.experimental import pallas as pl
from jax.experimental.pallas import tpu as pltpu
from jax.sharding import PartitionSpec as P

TILE = 128
NT = 16
ITERS = 4
NX = 4
N_ROW = 8
N_COL = 16
FRAMES = 128
RAYS = NT * TILE
VOX = NT * TILE
VP = VOX // N_ROW
RP = RAYS // N_COL
GROUPS = 2
M = FRAMES // GROUPS
MESH = pl.DeviceIdType.MESH
F32 = jnp.float32
BF16 = jnp.bfloat16

COL_PAIRS = (
    ((2, 2), (2, 1)),
    ((2, 3), (1, 2)),
    ((3, 2), (2, 0)),
    ((0, 2), (1, 1)),
    ((1, 3), (3, 1)),
    ((3, 3), (1, 0)),
    ((3, 0), (0, 1)),
    ((0, 3), (0, 0)),
)
COL_PEERS = tuple(d for pair in COL_PAIRS for d in pair)[:-1]
ROW_PEERS = tuple((dx, dc) for dx in (2, 1, 3, 0) for dc in (1, 0))[:-1]
X_PEERS = (2, 1, 3)
BATCHES = (2, 3, 3)
FIRST = 0.6


def frame_squares(x):
    total = None
    for i in range(x.shape[1] // 128):
        part = x[:, i * 128 : (i + 1) * 128].astype(F32)
        total = part * part if total is None else total + part * part
    if M < 128:
        total = jnp.concatenate([total, jnp.zeros((128 - M, 128), F32)], axis=0)
    return jnp.sum(total.T, axis=0, keepdims=True)


def per_frame(*rows):
    stack = jnp.concatenate([*rows, jnp.zeros((8 - len(rows), 128), F32)], axis=0).T
    return [stack[:M, i : i + 1] for i in range(len(rows))]


def kernel(
    slot_of, tiles, sino, vol_out, res_out,
    tl, tlt, a, at, u, v, dsend, drecv, rsend, rrecv, csend, crecv, own_r, own_c,
    s, d, im, vol, res, gam, step, guess, nr_send, nr_recv, ng_send, ng_recv, ni_send, ni_recv,
    tsem, u_ss, u_rs, v_ss, v_rs, f_ss, d_ss, d_rs, r_ss, r_rs, c_ss, c_rs, nr_ss, nr_rs, ng_ss, ng_rs, ni_ss, ni_rs,
):
    row = lax.axis_index("row")
    col = lax.axis_index("col")
    x, core = row // 2, row % 2
    y, z = col // 4, col % 4

    def row_of(dx, dc):
        return ((x + dx) % 4) * 2 + (core + dc) % 2

    def col_of(dy, dz):
        return ((y + dy) % 4) * 4 + (z + dz) % 4

    def remote(src, dst, ss, rs, to_row, to_col):
        return pltpu.make_async_remote_copy(
            src_ref=src, dst_ref=dst, send_sem=ss, recv_sem=rs, device_id=(to_row, to_col), device_id_type=MESH
        )

    def arrived(ref, sem):
        remote(ref, ref, sem, sem, row, col).wait_recv()

    def sent(ref, sem):
        remote(ref, ref, sem, sem, row, col).wait_send()

    n_col, n_row = len(COL_PEERS), len(ROW_PEERS)

    def send_field(g):
        for dy, dz in COL_PEERS:
            remote(u.at[g, col], u.at[g, col], u_ss.at[g], u_rs.at[g], row, col_of(dy, dz)).start()

    def send_norm(g, i_send, i_recv, ss, rs):
        for i, (dy, dz) in enumerate(COL_PEERS):
            remote(i_send.at[g], i_recv.at[g, i], ss.at[g], rs.at[g], row, col_of(dy, dz)).start()

    def send_row_norm(g):
        for i, (dx, dc) in enumerate(ROW_PEERS):
            remote(nr_send.at[g], nr_recv.at[g, i], nr_ss.at[g], nr_rs.at[g], row_of(dx, dc), col).start()

    def half(i):
        return pl.ds(2 * i, 2)

    def d_send(g, i):
        return remote(dsend.at[g, half(i)], drecv.at[g, half(i)], d_ss.at[g, i], d_rs.at[g, i], row_of(0, 1), col)

    def r_send(g, i):
        return remote(rsend.at[g, i], rrecv.at[g, i], r_ss.at[g], r_rs.at[g], row_of(X_PEERS[i], 0), col)

    def c_send(g, i):
        return remote(csend.at[g, i], crecv.at[g, i], c_ss.at[g], c_rs.at[g], row, col_of(*COL_PEERS[i]))

    def v_send(g, i):
        to = row_of(X_PEERS[i], 0) if i < 3 else row_of(0, 1)
        return remote(v.at[g, row], v.at[g, row], v_ss.at[g], v_rs.at[g, i], to, col)

    def f_send(g, i):
        slot = v.at[g, row_of(-X_PEERS[i], 0)]
        return remote(slot, slot, f_ss.at[g], v_rs.at[g, 3], row_of(0, 1), col)

    def voxel_product(field, n):
        block = a[:, pl.ds(pl.multiple_of(n * VP, VP), VP)]
        return jnp.dot(field, block, preferred_element_type=F32)

    def ray_product(field, first, second):
        columns = [at[:, pl.ds(pl.multiple_of(c * RP, RP), RP)] for c in (first, second)]
        return jnp.dot(field, jnp.concatenate(columns, axis=1), preferred_element_type=F32)

    def pass_norm(g):
        arrived(ni_recv.at[g, pl.ds(0, n_col)], ni_rs.at[g])
        squares = jnp.sum(ni_recv[g].reshape(N_COL, 128), axis=0, keepdims=True)
        nr_send[g] = squares
        nr_recv[g, n_row] = squares
        send_row_norm(g)
        sent(ni_recv.at[g, pl.ds(0, n_col)], ni_ss.at[g])

    def total_norm(g):
        arrived(nr_recv.at[g, pl.ds(0, n_row)], nr_rs.at[g])
        sent(nr_recv.at[g, pl.ds(0, n_row)], nr_ss.at[g])
        return jnp.sum(nr_recv[g].reshape(N_ROW, 128), axis=0, keepdims=True)

    def back_project(g):
        arrived(u.at[g, pl.ds(0, n_col)], u_rs.at[g])
        field = jnp.concatenate([u[g, i] for i in range(N_COL)], axis=1)
        order = (*X_PEERS, 0)
        for h in range(2):
            for i in (2 * h, 2 * h + 1):
                dsend[g, i] = voxel_product(field, row_of(order[i], 1)).astype(BF16)
            d_send(g, h).start()
        for i in range(4):
            own_r[g, i] = voxel_product(field, row_of(order[i], 0))
        pass_norm(g)
        for h in range(2):
            d_send(g, h).wait_recv()
            for i in (2 * h, 2 * h + 1):
                part = own_r[g, i] + drecv[g, i].astype(F32)
                if i < 3:
                    rsend[g, i] = part.astype(BF16)
                    r_send(g, i).start()
                else:
                    own_r[g, i] = part
        sent(u.at[g, pl.ds(0, n_col)], u_ss.at[g])

    def new_search(g, k):
        norm = total_norm(g)
        new_step = jnp.where(k == 0, FIRST * norm, gam[g] / norm)
        alpha, share = per_frame(new_step, jnp.where(k == 0, 1.0, new_step / guess[g]))
        step[g] = new_step
        arrived(rrecv.at[g], r_rs.at[g])
        total = own_r[g, 3]
        for i in range(3):
            total = total + rrecv[g, i].astype(F32)
        fresh = share * total + (1.0 - share) * s[g]
        s[g] = fresh
        v[g, row] = fresh.astype(BF16)
        for i in range(4):
            v_send(g, i).start()
        vol[g] = vol[g] + alpha * d[g]
        res[g] = res[g] - alpha * im[g]
        for h in range(2):
            d_send(g, h).wait_send()
        sent(rsend.at[g], r_ss.at[g])

    def project(g):
        for i in (1, 2, 0):
            slot = v.at[g, row_of(-X_PEERS[i], 0)]
            arrived(slot, v_rs.at[g, i])
            f_send(g, i).start()
        arrived(v.at[g, pl.ds(0, 4)], v_rs.at[g, 3])
        field = jnp.concatenate([v[g, i] for i in range(N_ROW)], axis=1)
        done = 0
        for many in BATCHES:
            for p in range(done, done + many):
                first, second = COL_PAIRS[p]
                part = ray_product(field, col_of(*first), col_of(*second))
                csend[g, 2 * p] = part[:, :RP].astype(BF16)
                if 2 * p + 1 < n_col:
                    csend[g, 2 * p + 1] = part[:, RP:].astype(BF16)
                else:
                    own_c[g] = part[:, RP:]
            if done == 0:
                squares = frame_squares(field)
                ng_send[g] = squares
                ng_recv[g, n_col] = squares
            for i in range(2 * done, min(2 * (done + many), n_col)):
                c_send(g, i).start()
            if done == 0:
                send_norm(g, ng_send, ng_recv, ng_ss, ng_rs)
            done += many
        sent(v.at[g, pl.ds(0, 4)], v_ss.at[g])
        sent(v.at[g, pl.ds(0, 3)], f_ss.at[g])

    def new_image(g, k):
        arrived(ng_recv.at[g, pl.ds(0, n_col)], ng_rs.at[g])
        gamma = jnp.sum(ng_recv[g].reshape(N_COL, 128), axis=0, keepdims=True)
        ahead = jnp.where(k == 0, step[g] / gamma, step[g])
        ahead = jnp.where((ahead > 1e-30) & (ahead < 1e30), ahead, 1.0)
        beta, trial = per_frame(jnp.where(k == 0, 0.0, gamma / gam[g]), ahead)
        gam[g] = gamma
        guess[g] = ahead
        arrived(crecv.at[g], c_rs.at[g])
        total = own_c[g]
        for i in range(n_col):
            total = total + crecv[g, i].astype(F32)
        image = total + beta * im[g]
        im[g] = image

        @pl.when(k + 1 < ITERS)
        def _():
            u[g, col] = (res[g] - trial * image).astype(BF16)
            send_field(g)

        squares = frame_squares(image)
        ni_send[g] = squares
        ni_recv[g, n_col] = squares
        send_norm(g, ni_send, ni_recv, ni_ss, ni_rs)
        d[g] = s[g] + beta * d[g]
        sent(csend.at[g], c_ss.at[g])
        sent(ng_recv.at[g, pl.ds(0, n_col)], ng_ss.at[g])

    load = pltpu.make_async_copy(tiles, tl.at[pl.ds(0, TILE)], tsem)
    load.start()
    barrier = pltpu.get_barrier_semaphore()
    for dy, dz in COL_PEERS:
        pl.semaphore_signal(barrier, inc=1, device_id=(row, col_of(dy, dz)), device_id_type=MESH)
    for dx, dc in ROW_PEERS:
        pl.semaphore_signal(barrier, inc=1, device_id=(row_of(dx, dc), col), device_id_type=MESH)
    first = sino[...].T
    for g in range(GROUPS):
        measured = first[g * M : (g + 1) * M]
        res[g] = measured
        u[g, col] = measured.astype(BF16)
        squares = frame_squares(measured)
        ni_send[g] = squares
        ni_recv[g, n_col] = squares
        s[g] = jnp.zeros((M, VP), F32)
        d[g] = jnp.zeros((M, VP), F32)
        vol[g] = jnp.zeros((M, VP), F32)
        im[g] = jnp.zeros((M, RP), F32)
        gam[g] = jnp.ones((1, 128), F32)
        guess[g] = jnp.ones((1, 128), F32)
    tl[TILE] = jnp.zeros((TILE, TILE), BF16)
    pl.semaphore_wait(barrier, n_col + n_row)
    for g in range(GROUPS):
        send_field(g)
        send_norm(g, ni_send, ni_recv, ni_ss, ni_rs)
    load.wait()

    def place(i, carry):
        for j in range(NT):
            rows = pl.ds(pl.multiple_of(i * TILE, TILE), TILE)
            a[rows, j * TILE : (j + 1) * TILE] = tl[slot_of[i * NT + j]]
        return carry

    lax.fori_loop(0, NT, place, 0)

    def turn():
        def one(t, carry):
            for i in range(8):
                tlt[t * 8 + i] = tl[t * 8 + i].T
            return carry

        lax.fori_loop(0, TILE // 8, one, 0)
        tlt[TILE] = jnp.zeros((TILE, TILE), BF16)

        def place_turned(i, carry):
            for j in range(NT):
                columns = pl.ds(pl.multiple_of(i * TILE, TILE), TILE)
                at[j * TILE : (j + 1) * TILE, columns] = tlt[slot_of[i * NT + j]]
            return carry

        lax.fori_loop(0, NT, place_turned, 0)

    def iteration(k, carry):
        back_project(0)

        @pl.when(k == 0)
        def _():
            turn()

        if GROUPS == 1:
            new_search(0, k)
            project(0)
            new_image(0, k)
            return carry

        @pl.when(k > 0)
        def _():
            new_image(1, k - 1)

        new_search(0, k)
        back_project(1)
        project(0)
        new_search(1, k)
        new_image(0, k)
        project(1)
        return carry

    lax.fori_loop(0, ITERS, iteration, 0)

    def finish(g):
        (alpha,) = per_frame(gam[g] / total_norm(g))
        return vol[g] + alpha * d[g], res[g] - alpha * im[g]

    if GROUPS == 2:
        new_image(1, ITERS - 1)
    done = []
    for g in range(GROUPS):
        pass_norm(g)
    for g in range(GROUPS):
        done.append(finish(g))
    vol_out[...] = jnp.concatenate([volume for volume, _ in done], axis=0).T
    res_out[...] = jnp.concatenate([residual for _, residual in done], axis=0).T


def local(tiles, tile_row, tile_col, tile_count, sinogram):
    live = jnp.arange(TILE, dtype=jnp.int32) < tile_count[0, 0]
    place = jnp.where(live, tile_row[0, 0] * NT + tile_col[0, 0], -1)
    slots = jnp.arange(TILE, dtype=jnp.int32)
    here = place[None, :] == jnp.arange(NT * NT, dtype=jnp.int32)[:, None]
    slot_of = jnp.min(jnp.where(here, slots[None, :], TILE), axis=1)
    dma = pltpu.SemaphoreType.DMA
    vm = pltpu.VMEM
    G, nc = GROUPS, len(COL_PEERS)
    volume, residual = pl.pallas_call(
        kernel,
        out_shape=(jax.ShapeDtypeStruct((VP, FRAMES), F32), jax.ShapeDtypeStruct((RP, FRAMES), F32)),
        in_specs=[
            pl.BlockSpec(memory_space=pltpu.SMEM),
            pl.BlockSpec(memory_space=pl.ANY),
            pl.BlockSpec(memory_space=pltpu.VMEM),
        ],
        out_specs=(pl.BlockSpec(memory_space=pltpu.VMEM), pl.BlockSpec(memory_space=pltpu.VMEM)),
        scratch_shapes=[
            vm((TILE + 1, TILE, TILE), BF16), vm((TILE + 1, TILE, TILE), BF16),
            vm((RAYS, VOX), BF16), vm((VOX, RAYS), BF16),
            vm((G, N_COL, M, RP), BF16), vm((G, N_ROW, M, VP), BF16),
            vm((G, 4, M, VP), BF16), vm((G, 4, M, VP), BF16), vm((G, 3, M, VP), BF16), vm((G, 3, M, VP), BF16),
            vm((G, nc, M, RP), BF16), vm((G, nc, M, RP), BF16),
            vm((G, 4, M, VP), F32), vm((G, M, RP), F32),
            vm((G, M, VP), F32), vm((G, M, VP), F32), vm((G, M, RP), F32), vm((G, M, VP), F32), vm((G, M, RP), F32),
            vm((G, 1, 128), F32), vm((G, 1, 128), F32), vm((G, 1, 128), F32),
            vm((G, 1, 128), F32), vm((G, N_ROW, 1, 128), F32),
            vm((G, 1, 128), F32), vm((G, N_COL, 1, 128), F32), vm((G, 1, 128), F32), vm((G, N_COL, 1, 128), F32),
            dma, dma((G,)), dma((G,)), dma((G,)), dma((G, 4)), dma((G,)), dma((G, 2)), dma((G, 2)), dma((G,)), dma((G,)),
            dma((G,)), dma((G,)), dma((G,)), dma((G,)), dma((G,)), dma((G,)), dma((G,)), dma((G,)),
        ],
        compiler_params=pltpu.CompilerParams(
            collective_id=0, has_side_effects=True, vmem_limit_bytes=60 * 1024 * 1024
        ),
    )(slot_of, tiles[0, 0], sinogram[0])
    return (volume[None], residual[None])


def solution(mesh):
    placed = (
        P("row", "col", None, None, None),
        P("row", "col", None),
        P("row", "col", None),
        P("row", "col"),
        P("row", "col", None),
    )
    return jax.shard_map(
        local,
        mesh=mesh,
        in_specs=placed,
        out_specs=(P("col", "row", None), P("row", "col", None)),
        check_vma=False,
    )
```

time: 698 us -> 135 us (0.19); the launches traced: 684 us -> 134 us
  blocking collectives: 430 us -> 0 us
  Pallas kernels: 0 us -> 129 us
  matrix products: 114 us -> 0 us
  local copies, waits for them, and re-layouts: 104 us -> 3.04 us
  waiting for transfers between devices: 17.7 us -> 0 us
  starting transfers between devices: 13 us -> 0 us
    all_to_all x14 -> x0, blocking collectives: 247 us -> none  [the longest x8 164 us: sum_at_owner(): lax.all_to_all(parts, axis, split_axis=0, concat_axis=0, tiled=True)]
    psum x28 -> x0, blocking collectives: 182 us -> none  [by_axis(): return functools.reduce(lax.psum, axes, shard)]
    pallas_call x0 -> x1, Pallas kernels: none -> 129 us  [local(): pl.pallas_call(kernel, out_shape=(jax.ShapeDtypeStruct((VP, FRAMES), F32)...]
    dot_general x16 -> x0, matrix products: 114 us -> none  [the longest x4 39.6 us: forward_local(): jnp.einsum('tij,tjk->tik', blocks, picked, preferred_element_type=jnp.flo...]
    dot_general x12 -> x0, local copies, waits for them, and re-layouts: 75.5 us -> none  [the longest x4 37.1 us: backward_local(): jnp.einsum('tji,tjk->tik', blocks, picked, preferred_element_type=jnp.flo...]
    gather x8 -> x0, local copies, waits for them, and re-layouts: 24.5 us -> none  [the longest x4 12.2 us: forward_local(): picked = jnp.take(voxel_tiles, cols_index, axis=0)]
    all_to_all x2 -> x0, waiting for transfers between devices: 17.7 us -> none  [sent_to_all(): return lax.all_to_all(copies, axis, split_axis=0, concat_axis=0, tiled=True)]
    all_to_all x2 -> x0, starting transfers between devices: 13 us -> none  [sent_to_all(): return lax.all_to_all(copies, axis, split_axis=0, concat_axis=0, tiled=True)]
  transfers between devices with their start and end apart: 2 -> 0, of which waited for: 2 -> 0; matrix products, arithmetic and copies ran while one was open for 0% -> 0% of each run, Pallas kernels for 0% -> 0%
where the time goes in v1:
time: 135 us; the launch traced here: 134 us
  Pallas kernels  129 us (96%)
  local copies, waits for them, and re-layouts  3.04 us (2%)
  other arithmetic  1.36 us (1%)
    pallas_call x1, Pallas kernels, local(): pl.pallas_call(kernel, out_shape=(jax.ShapeDtypeStruct((VP, FRAMES), F32)...  129 us
    unnamed x2, local copies, waits for them, and re-layouts  3.04 us

profile of v1, /device:TPU:1, one launch (start us, length us, event | category | flops | bytes accessed | tf_op | source)
XLA Modules:
  0.0 134.3 jit_solution(15594654312366960524)
XLA Ops:
  1.3 0.7 compare_select_fusion
  2.0 0.7 select_reduce_fusion.slot_of
  2.6 128.6 %shard_map.68 = (f32[256,128]{1,0:T(8,128)}, f32[128,128]{1,0:T(8,128)}) custom-call(s32[256]{0:T(256)} %select_reduce_fusion.slot_of, bf16[128,128,128]{2,1,0:T(8,128)(2,1)} %bitcast.8, f32[128,128]{1,0:T(8,128)} %bitcast.10), custom_call_target="tpu_custom_call" | custom-call | tf_op jit(solution)/shard_map/pallas_call | solution.py:345
  131.3 1.6 %copy.10 = f32[1,256,128]{2,1,0:T(8,128)} copy(f32[1,256,128]{2,1,0:T(8,128)} %bitcast.9) | data formatting | bytes 262144
  132.9 1.5 %copy.11 = f32[1,128,128]{2,1,0:T(8,128)} copy(f32[1,128,128]{2,1,0:T(8,128)} %bitcast.11) | data formatting | bytes 131072

commit v2 on v1

--- a/solution.py
+++ b/solution.py
@@ -36,7 +36,7 @@
 )
 COL_PEERS = tuple(d for pair in COL_PAIRS for d in pair)[:-1]
 ROW_PEERS = tuple((dx, dc) for dx in (2, 1, 3, 0) for dc in (1, 0))[:-1]
-X_PEERS = (2, 1, 3)
+BACK_BATCHES = (2, 3, 3)
 BATCHES = (2, 3, 3)
 FIRST = 0.6
 
@@ -58,9 +58,9 @@
 
 def kernel(
     slot_of, tiles, sino, vol_out, res_out,
-    tl, tlt, a, at, u, v, dsend, drecv, rsend, rrecv, csend, crecv, own_r, own_c,
+    tl, a, at, u, v, rsend, rrecv, csend, crecv, own_r, own_c,
     s, d, im, vol, res, gam, step, guess, nr_send, nr_recv, ng_send, ng_recv, ni_send, ni_recv,
-    tsem, u_ss, u_rs, v_ss, v_rs, f_ss, d_ss, d_rs, r_ss, r_rs, c_ss, c_rs, nr_ss, nr_rs, ng_ss, ng_rs, ni_ss, ni_rs,
+    tsem, u_ss, u_rs, v_ss, v_rs, r_ss, r_rs, c_ss, c_rs, nr_ss, nr_rs, ng_ss, ng_rs, ni_ss, ni_rs,
 ):
     row = lax.axis_index("row")
     col = lax.axis_index("col")
@@ -98,33 +98,23 @@
         for i, (dx, dc) in enumerate(ROW_PEERS):
             remote(nr_send.at[g], nr_recv.at[g, i], nr_ss.at[g], nr_rs.at[g], row_of(dx, dc), col).start()
 
-    def half(i):
-        return pl.ds(2 * i, 2)
-
-    def d_send(g, i):
-        return remote(dsend.at[g, half(i)], drecv.at[g, half(i)], d_ss.at[g, i], d_rs.at[g, i], row_of(0, 1), col)
-
     def r_send(g, i):
-        return remote(rsend.at[g, i], rrecv.at[g, i], r_ss.at[g], r_rs.at[g], row_of(X_PEERS[i], 0), col)
+        return remote(rsend.at[g, i], rrecv.at[g, i], r_ss.at[g], r_rs.at[g], row_of(*ROW_PEERS[i]), col)
 
     def c_send(g, i):
         return remote(csend.at[g, i], crecv.at[g, i], c_ss.at[g], c_rs.at[g], row, col_of(*COL_PEERS[i]))
 
-    def v_send(g, i):
-        to = row_of(X_PEERS[i], 0) if i < 3 else row_of(0, 1)
-        return remote(v.at[g, row], v.at[g, row], v_ss.at[g], v_rs.at[g, i], to, col)
-
-    def f_send(g, i):
-        slot = v.at[g, row_of(-X_PEERS[i], 0)]
-        return remote(slot, slot, f_ss.at[g], v_rs.at[g, 3], row_of(0, 1), col)
+    def send_search(g):
+        for dx, dc in ROW_PEERS:
+            remote(v.at[g, row], v.at[g, row], v_ss.at[g], v_rs.at[g], row_of(dx, dc), col).start()
 
     def voxel_product(field, n):
-        block = a[:, pl.ds(pl.multiple_of(n * VP, VP), VP)]
+        block = jnp.concatenate([a[2 * n], a[2 * n + 1]], axis=1)
         return jnp.dot(field, block, preferred_element_type=F32)
 
     def ray_product(field, first, second):
-        columns = [at[:, pl.ds(pl.multiple_of(c * RP, RP), RP)] for c in (first, second)]
-        return jnp.dot(field, jnp.concatenate(columns, axis=1), preferred_element_type=F32)
+        block = jnp.concatenate([at[first], at[second]], axis=1)
+        return jnp.dot(field, block, preferred_element_type=F32)
 
     def pass_norm(g):
         arrived(ni_recv.at[g, pl.ds(0, n_col)], ni_rs.at[g])
@@ -142,23 +132,18 @@
     def back_project(g):
         arrived(u.at[g, pl.ds(0, n_col)], u_rs.at[g])
         field = jnp.concatenate([u[g, i] for i in range(N_COL)], axis=1)
-        order = (*X_PEERS, 0)
-        for h in range(2):
-            for i in (2 * h, 2 * h + 1):
-                dsend[g, i] = voxel_product(field, row_of(order[i], 1)).astype(BF16)
-            d_send(g, h).start()
-        for i in range(4):
-            own_r[g, i] = voxel_product(field, row_of(order[i], 0))
-        pass_norm(g)
-        for h in range(2):
-            d_send(g, h).wait_recv()
-            for i in (2 * h, 2 * h + 1):
-                part = own_r[g, i] + drecv[g, i].astype(F32)
-                if i < 3:
-                    rsend[g, i] = part.astype(BF16)
-                    r_send(g, i).start()
+        done = 0
+        for many in BACK_BATCHES:
+            for i in range(done, done + many):
+                if i < n_row:
+                    rsend[g, i] = voxel_product(field, row_of(*ROW_PEERS[i])).astype(BF16)
                 else:
-                    own_r[g, i] = part
+                    own_r[g] = voxel_product(field, row)
+            for i in range(done, min(done + many, n_row)):
+                r_send(g, i).start()
+            if done == 0:
+                pass_norm(g)
+            done += many
         sent(u.at[g, pl.ds(0, n_col)], u_ss.at[g])
 
     def new_search(g, k):
@@ -167,26 +152,19 @@
         alpha, share = per_frame(new_step, jnp.where(k == 0, 1.0, new_step / guess[g]))
         step[g] = new_step
         arrived(rrecv.at[g], r_rs.at[g])
-        total = own_r[g, 3]
-        for i in range(3):
+        total = own_r[g]
+        for i in range(n_row):
             total = total + rrecv[g, i].astype(F32)
         fresh = share * total + (1.0 - share) * s[g]
         s[g] = fresh
         v[g, row] = fresh.astype(BF16)
-        for i in range(4):
-            v_send(g, i).start()
+        send_search(g)
         vol[g] = vol[g] + alpha * d[g]
         res[g] = res[g] - alpha * im[g]
-        for h in range(2):
-            d_send(g, h).wait_send()
         sent(rsend.at[g], r_ss.at[g])
 
     def project(g):
-        for i in (1, 2, 0):
-            slot = v.at[g, row_of(-X_PEERS[i], 0)]
-            arrived(slot, v_rs.at[g, i])
-            f_send(g, i).start()
-        arrived(v.at[g, pl.ds(0, 4)], v_rs.at[g, 3])
+        arrived(v.at[g, pl.ds(0, n_row)], v_rs.at[g])
         field = jnp.concatenate([v[g, i] for i in range(N_ROW)], axis=1)
         done = 0
         for many in BATCHES:
@@ -207,8 +185,7 @@
             if done == 0:
                 send_norm(g, ng_send, ng_recv, ng_ss, ng_rs)
             done += many
-        sent(v.at[g, pl.ds(0, 4)], v_ss.at[g])
-        sent(v.at[g, pl.ds(0, 3)], f_ss.at[g])
+        sent(v.at[g, pl.ds(0, n_row)], v_ss.at[g])
 
     def new_image(g, k):
         arrived(ng_recv.at[g, pl.ds(0, n_col)], ng_rs.at[g])
@@ -269,27 +246,25 @@
     def place(i, carry):
         for j in range(NT):
             rows = pl.ds(pl.multiple_of(i * TILE, TILE), TILE)
-            a[rows, j * TILE : (j + 1) * TILE] = tl[slot_of[i * NT + j]]
+            a[j, rows, :] = tl[slot_of[i * NT + j]]
         return carry
 
     lax.fori_loop(0, NT, place, 0)
 
     def turn():
-        def one(t, carry):
-            for i in range(8):
-                tlt[t * 8 + i] = tl[t * 8 + i].T
+        places = [lax.broadcasted_iota(jnp.int32, (2 * TILE, 2 * TILE), i) for i in range(2)]
+        one = jnp.where(places[0] == places[1], 1.0, 0.0).astype(BF16)
+
+        def rows(i, carry):
+            here = pl.ds(pl.multiple_of(i * 2 * TILE, 2 * TILE), 2 * TILE)
+            for j in range(NT // 2):
+                block = jnp.concatenate([a[2 * j, here, :], a[2 * j + 1, here, :]], axis=1)
+                turned = lax.dot_general(one, block, (((1,), (1,)), ((), ())), preferred_element_type=F32).astype(BF16)
+                at[2 * i, j * 2 * TILE : (j + 1) * 2 * TILE, :] = turned[:, :TILE]
+                at[2 * i + 1, j * 2 * TILE : (j + 1) * 2 * TILE, :] = turned[:, TILE:]
             return carry
 
-        lax.fori_loop(0, TILE // 8, one, 0)
-        tlt[TILE] = jnp.zeros((TILE, TILE), BF16)
-
-        def place_turned(i, carry):
-            for j in range(NT):
-                columns = pl.ds(pl.multiple_of(i * TILE, TILE), TILE)
-                at[j * TILE : (j + 1) * TILE, columns] = tlt[slot_of[i * NT + j]]
-            return carry
-
-        lax.fori_loop(0, NT, place_turned, 0)
+        lax.fori_loop(0, NT // 2, rows, 0)
 
     def iteration(k, carry):
         back_project(0)
@@ -341,7 +316,7 @@
     slot_of = jnp.min(jnp.where(here, slots[None, :], TILE), axis=1)
     dma = pltpu.SemaphoreType.DMA
     vm = pltpu.VMEM
-    G, nc = GROUPS, len(COL_PEERS)
+    G, nc, nr = GROUPS, len(COL_PEERS), len(ROW_PEERS)
     volume, residual = pl.pallas_call(
         kernel,
         out_shape=(jax.ShapeDtypeStruct((VP, FRAMES), F32), jax.ShapeDtypeStruct((RP, FRAMES), F32)),
@@ -352,17 +327,17 @@
         ],
         out_specs=(pl.BlockSpec(memory_space=pltpu.VMEM), pl.BlockSpec(memory_space=pltpu.VMEM)),
         scratch_shapes=[
-            vm((TILE + 1, TILE, TILE), BF16), vm((TILE + 1, TILE, TILE), BF16),
-            vm((RAYS, VOX), BF16), vm((VOX, RAYS), BF16),
+            vm((TILE + 1, TILE, TILE), BF16),
+            vm((NT, RAYS, TILE), BF16), vm((NT, VOX, TILE), BF16),
             vm((G, N_COL, M, RP), BF16), vm((G, N_ROW, M, VP), BF16),
-            vm((G, 4, M, VP), BF16), vm((G, 4, M, VP), BF16), vm((G, 3, M, VP), BF16), vm((G, 3, M, VP), BF16),
+            vm((G, nr, M, VP), BF16), vm((G, nr, M, VP), BF16),
             vm((G, nc, M, RP), BF16), vm((G, nc, M, RP), BF16),
-            vm((G, 4, M, VP), F32), vm((G, M, RP), F32),
+            vm((G, M, VP), F32), vm((G, M, RP), F32),
             vm((G, M, VP), F32), vm((G, M, VP), F32), vm((G, M, RP), F32), vm((G, M, VP), F32), vm((G, M, RP), F32),
             vm((G, 1, 128), F32), vm((G, 1, 128), F32), vm((G, 1, 128), F32),
             vm((G, 1, 128), F32), vm((G, N_ROW, 1, 128), F32),
             vm((G, 1, 128), F32), vm((G, N_COL, 1, 128), F32), vm((G, 1, 128), F32), vm((G, N_COL, 1, 128), F32),
-            dma, dma((G,)), dma((G,)), dma((G,)), dma((G, 4)), dma((G,)), dma((G, 2)), dma((G, 2)), dma((G,)), dma((G,)),
+            dma, dma((G,)), dma((G,)), dma((G,)), dma((G,)), dma((G,)), dma((G,)),
             dma((G,)), dma((G,)), dma((G,)), dma((G,)), dma((G,)), dma((G,)), dma((G,)), dma((G,)),
         ],
         compiler_params=pltpu.CompilerParams(

time: 135 us -> 129 us (0.956)
  Pallas kernels: 129 us -> 123 us
    pallas_call x1, Pallas kernels: 129 us -> 123 us  [local(): pl.pallas_call(kernel, out_shape=(jax.ShapeDtypeStruct((VP, FRAMES), F32)...]
where the time goes in v2:
time: 129 us
  Pallas kernels  123 us (95%)
  local copies, waits for them, and re-layouts  3.04 us (2%)
  other arithmetic  1.36 us (1%)
  between operations  1.29 us (1%)
    pallas_call x1, Pallas kernels, local(): pl.pallas_call(kernel, out_shape=(jax.ShapeDtypeStruct((VP, FRAMES), F32)...  123 us
    unnamed x2, local copies, waits for them, and re-layouts  3.04 us

profile of v2, /device:TPU:1, one launch (start us, length us, event | category | flops | bytes accessed | tf_op | source)
XLA Modules:
  0.0 128.8 jit_solution(15854908196481216962)
XLA Ops:
  1.3 0.7 compare_select_fusion
  2.0 0.7 select_reduce_fusion.slot_of
  2.6 123.1 %shard_map.68 = (f32[256,128]{1,0:T(8,128)}, f32[128,128]{1,0:T(8,128)}) custom-call(s32[256]{0:T(256)} %select_reduce_fusion.slot_of, bf16[128,128,128]{2,1,0:T(8,128)(2,1)} %bitcast.8, f32[128,128]{1,0:T(8,128)} %bitcast.10), custom_call_target="tpu_custom_call" | custom-call | tf_op jit(solution)/shard_map/pallas_call | solution.py:320
  125.7 1.6 %copy.10 = f32[1,256,128]{2,1,0:T(8,128)} copy(f32[1,256,128]{2,1,0:T(8,128)} %bitcast.9) | data formatting | bytes 262144
  127.3 1.5 %copy.11 = f32[1,128,128]{2,1,0:T(8,128)} copy(f32[1,128,128]{2,1,0:T(8,128)} %bitcast.11) | data formatting | bytes 131072

commit v3 on v2

--- a/solution.py
+++ b/solution.py
@@ -57,10 +57,10 @@
 
 
 def kernel(
-    slot_of, tiles, sino, vol_out, res_out,
-    tl, a, at, u, v, rsend, rrecv, csend, crecv, own_r, own_c,
+    slots, tiles, sinogram, vol_out, res_out,
+    slot_of, sino, tl, a, at, u, v, rsend, rrecv, csend, crecv, own_r, own_c,
     s, d, im, vol, res, gam, step, guess, nr_send, nr_recv, ng_send, ng_recv, ni_send, ni_recv,
-    tsem, u_ss, u_rs, v_ss, v_rs, r_ss, r_rs, c_ss, c_rs, nr_ss, nr_rs, ng_ss, ng_rs, ni_ss, ni_rs,
+    tsem, ssem, isem, u_ss, u_rs, v_ss, v_rs, r_ss, r_rs, c_ss, c_rs, nr_ss, nr_rs, ng_ss, ng_rs, ni_ss, ni_rs,
 ):
     row = lax.axis_index("row")
     col = lax.axis_index("col")
@@ -215,13 +215,18 @@
         sent(csend.at[g], c_ss.at[g])
         sent(ng_recv.at[g, pl.ds(0, n_col)], ng_ss.at[g])
 
-    load = pltpu.make_async_copy(tiles, tl.at[pl.ds(0, TILE)], tsem)
-    load.start()
     barrier = pltpu.get_barrier_semaphore()
     for dy, dz in COL_PEERS:
         pl.semaphore_signal(barrier, inc=1, device_id=(row, col_of(dy, dz)), device_id_type=MESH)
     for dx, dc in ROW_PEERS:
         pl.semaphore_signal(barrier, inc=1, device_id=(row_of(dx, dc), col), device_id_type=MESH)
+    measure = pltpu.make_async_copy(sinogram, sino, ssem)
+    measure.start()
+    listed = pltpu.make_async_copy(slots, slot_of, isem)
+    listed.start()
+    load = pltpu.make_async_copy(tiles, tl.at[pl.ds(0, TILE)], tsem)
+    load.start()
+    measure.wait()
     first = sino[...].T
     for g in range(GROUPS):
         measured = first[g * M : (g + 1) * M]
@@ -241,6 +246,7 @@
     for g in range(GROUPS):
         send_field(g)
         send_norm(g, ni_send, ni_recv, ni_ss, ni_rs)
+    listed.wait()
     load.wait()
 
     def place(i, carry):
@@ -306,6 +312,11 @@
         done.append(finish(g))
     vol_out[...] = jnp.concatenate([volume for volume, _ in done], axis=0).T
     res_out[...] = jnp.concatenate([residual for _, residual in done], axis=0).T
+
+
+def hand_over(vol_in, res_in, vol_out, res_out):
+    vol_out[0] = vol_in[...]
+    res_out[0] = res_in[...]
 
 
 def local(tiles, tile_row, tile_col, tile_count, sinogram):
@@ -321,12 +332,13 @@
         kernel,
         out_shape=(jax.ShapeDtypeStruct((VP, FRAMES), F32), jax.ShapeDtypeStruct((RP, FRAMES), F32)),
         in_specs=[
-            pl.BlockSpec(memory_space=pltpu.SMEM),
             pl.BlockSpec(memory_space=pl.ANY),
-            pl.BlockSpec(memory_space=pltpu.VMEM),
+            pl.BlockSpec(memory_space=pl.ANY),
+            pl.BlockSpec(memory_space=pl.ANY),
         ],
         out_specs=(pl.BlockSpec(memory_space=pltpu.VMEM), pl.BlockSpec(memory_space=pltpu.VMEM)),
         scratch_shapes=[
+            pltpu.SMEM((NT * NT,), jnp.int32), vm((RP, FRAMES), F32),
             vm((TILE + 1, TILE, TILE), BF16),
             vm((NT, RAYS, TILE), BF16), vm((NT, VOX, TILE), BF16),
             vm((G, N_COL, M, RP), BF16), vm((G, N_ROW, M, VP), BF16),
@@ -337,14 +349,17 @@
             vm((G, 1, 128), F32), vm((G, 1, 128), F32), vm((G, 1, 128), F32),
             vm((G, 1, 128), F32), vm((G, N_ROW, 1, 128), F32),
             vm((G, 1, 128), F32), vm((G, N_COL, 1, 128), F32), vm((G, 1, 128), F32), vm((G, N_COL, 1, 128), F32),
-            dma, dma((G,)), dma((G,)), dma((G,)), dma((G,)), dma((G,)), dma((G,)),
+            dma, dma, dma, dma((G,)), dma((G,)), dma((G,)), dma((G,)), dma((G,)), dma((G,)),
             dma((G,)), dma((G,)), dma((G,)), dma((G,)), dma((G,)), dma((G,)), dma((G,)), dma((G,)),
         ],
         compiler_params=pltpu.CompilerParams(
             collective_id=0, has_side_effects=True, vmem_limit_bytes=60 * 1024 * 1024
         ),
     )(slot_of, tiles[0, 0], sinogram[0])
-    return (volume[None], residual[None])
+    return pl.pallas_call(
+        hand_over,
+        out_shape=(jax.ShapeDtypeStruct((1, VP, FRAMES), F32), jax.ShapeDtypeStruct((1, RP, FRAMES), F32)),
+    )(volume, residual)
 
 
 def solution(mesh):

time: 129 us -> 127 us (0.984)
  local copies, waits for them, and re-layouts: 3.04 us -> 0 us
    unnamed x2 -> x0, local copies, waits for them, and re-layouts: 3.04 us -> none
    pallas_call x0 -> x1, Pallas kernels: none -> 1.59 us  [local(): pl.pallas_call(hand_over, out_shape=(jax.ShapeDtypeStruct((1, VP, FRAMES)...]
where the time goes in v3:
time: 127 us
  Pallas kernels  124 us (98%)
  other arithmetic  1.36 us (1%)
  between operations  1.29 us (1%)
    pallas_call x1, Pallas kernels, local(): pl.pallas_call(kernel, out_shape=(jax.ShapeDtypeStruct((VP, FRAMES), F32)...  122 us

profile of v3, /device:TPU:1, one launch (start us, length us, event | category | flops | bytes accessed | tf_op | source)
XLA Modules:
  0.0 126.5 jit_solution(8659452267475634790)
XLA Ops:
  1.3 0.7 compare_select_fusion
  2.0 0.7 select_reduce_fusion.slots
  2.6 122.3 %shard_map.68 = (f32[256,128]{1,0:T(8,128)}, f32[128,128]{1,0:T(8,128)}) custom-call(s32[256]{0:T(256)} %select_reduce_fusion.slots, bf16[128,128,128]{2,1,0:T(8,128)(2,1)} %bitcast.6, f32[128,128]{1,0:T(8,128)} %bitcast.7), custom_call_target="tpu_custom_call" | custom-call | tf_op jit(solution)/shard_map/pallas_call | solution.py:331
  124.9 1.6 %shard_map.69 = (f32[1,256,128]{2,1,0:T(8,128)}, f32[1,128,128]{2,1,0:T(8,128)}) custom-call(f32[256,128]{1,0:T(8,128)} %get-tuple-element.4.vol_in, f32[128,128]{1,0:T(8,128)} %get-tuple-element.5.res_in), custom_call_target="tpu_custom_call" | custom-call | tf_op jit(solution)/shard_map/pallas_call | solution.py:359
